TPU v7x, 32 devices: a whole 2x2x4 slice. The times are simulated.
32 devices in a mesh: seq: 8 (over y, x, core), tp: 4 (over z).
Axes of the slice: x: 2, y: 2, z: 4, core: 2. Of those that a mesh axis runs over, the one named last changes fastest.
Arguments:
- hidden_in: bfloat16 [4096, 2048], P('seq', 'tp'), may hold values from -60 to 60
- w_query: bfloat16 [2048, 2048], P(None, 'tp'), may hold values from -0.125 to 0.125
- w_key: bfloat16 [2048, 2048], P(None, 'tp'), may hold values from -0.125 to 0.125
- w_value: bfloat16 [2048, 2048], P(None, 'tp'), may hold values from -0.8984375 to 0.8984375
- w_pos: bfloat16 [2048, 2048], P(None, 'tp'), may hold values from -0.125 to 0.125
- w_out: bfloat16 [2048, 2048], P('tp'), may hold values from -0.125 to 0.125
- bias_content: float32 [16, 128], P('tp'), may hold values from -4 to 4
- bias_pos: float32 [16, 128], P('tp'), may hold values from -4 to 4
- norm_gain: float32 [2048], P('tp'), may hold values from 0.1 to 1.9
- norm_bias: float32 [2048], P('tp'), may hold values from -3 to 3
Outputs:
- hidden_out: bfloat16 [4096, 2048], P('seq', 'tp')
All inputs are finite; a program needn't handle non-finite values.
Results may differ from a plain program's by a relative error of at most 0.014.
The roundings to bfloat16 on the way count: a program that leaves them out, or rounds other values in their place, can miss the bound.
Values may be sent and summed in bfloat16 or wider, within the bound.
No kernel may reach another device: no remote copies, remote signals or barrier semaphores. Data moves between devices by JAX's collectives and lax.ppermute only.
A program may use at most 128 MiB of HBM per device.

v0:
```python
import jax
import jax.numpy as jnp
from jax import lax
from jax.sharding import PartitionSpec as P


def shifted(block, axis, distance):
    devices = range(lax.axis_size(axis))
    route = [(i - distance, i) for i in devices if i - distance in devices]
    return lax.ppermute(block, axis, route)


def relative_table(span, width):
    half = width // 2
    freq = jnp.exp(-jnp.log(10000.0) * jnp.arange(half).astype(jnp.float32) / half)
    distance = (span - 1 - jnp.arange(span)).astype(jnp.float32)
    angle = distance[:, None] * freq[None, :]
    return jnp.concatenate([jnp.sin(angle), jnp.cos(angle)], 1).astype(jnp.bfloat16)


def shift_rows(table, seg, span):
    heads = table.shape[0]
    padded = jnp.pad(table, ((0, 0), (0, 0), (0, 1)))
    flat = padded.reshape(heads, seg * (span + 1))
    return flat[:, seg - 1 : seg - 1 + seg * span].reshape(heads, seg, span)


def shards(
    hidden_in, w_query, w_key, w_value, w_pos, w_out, bias_content, bias_pos, norm_gain, norm_bias
):
    seg = hidden_in.shape[0]
    heads = bias_content.shape[0]
    head_dim = bias_content.shape[1]
    width = heads * head_dim
    model_width = w_query.shape[0]
    span = 3 * seg
    memory = 2 * seg
    place = lax.axis_index("seq")
    own = lax.all_gather(hidden_in, "tp", axis=1, tiled=True)
    query = jnp.dot(own, w_query, preferred_element_type=jnp.float32).astype(jnp.bfloat16)
    own_keys = jnp.dot(own, w_key, preferred_element_type=jnp.float32).astype(jnp.bfloat16)
    own_values = jnp.dot(own, w_value, preferred_element_type=jnp.float32).astype(jnp.bfloat16)
    key_parts = []
    value_parts = []
    for distance in (2, 1):
        earlier_keys, earlier_values = shifted((own_keys, own_values), "seq", distance)
        key_parts.append(earlier_keys)
        value_parts.append(earlier_values)
    keys = jnp.concatenate(key_parts + [own_keys], 0)
    values = jnp.concatenate(value_parts + [own_values], 0)
    rel = jnp.dot(
        relative_table(span, model_width), w_pos, preferred_element_type=jnp.float32
    ).astype(jnp.bfloat16)
    rel = rel.reshape(span, heads, head_dim)
    keys = keys.reshape(span, heads, head_dim)
    values = values.reshape(span, heads, head_dim)
    q_rows = query.astype(jnp.float32).reshape(seg, heads, head_dim)
    content_q = (q_rows + bias_content[None]).astype(jnp.bfloat16)
    pos_q = (q_rows + bias_pos[None]).astype(jnp.bfloat16)
    content = jnp.einsum("ihd,jhd->hij", content_q, keys, preferred_element_type=jnp.float32)
    position = jnp.einsum("ihd,ehd->hie", pos_q, rel, preferred_element_type=jnp.float32)
    position = shift_rows(position, seg, span)
    score = (content + position) * (1.0 / jnp.sqrt(jnp.float32(head_dim)))
    row = jnp.arange(seg)[:, None]
    col = jnp.arange(span)[None, :]
    allowed = (col <= row + memory) & (place * seg - memory + col >= 0)
    score = jnp.where(allowed[None], score, jnp.float32(-1e30))
    probs = jax.nn.softmax(score, axis=-1).astype(jnp.bfloat16)
    attended = jnp.einsum("hij,jhd->ihd", probs, values, preferred_element_type=jnp.float32)
    attended = attended.astype(jnp.bfloat16).reshape(seg, width)
    partial_out = jnp.dot(attended, w_out, preferred_element_type=jnp.float32)
    branch = lax.psum_scatter(
        partial_out.astype(jnp.bfloat16), "tp", scatter_dimension=1, tiled=True
    ).astype(jnp.float32)
    summed = hidden_in.astype(jnp.float32) + branch
    total = lax.psum(jnp.sum(summed, axis=1), "tp")
    center = total / model_width
    centred = summed - center[:, None]
    spread = lax.psum(jnp.sum(centred * centred, axis=1), "tp") / model_width
    normed = centred / jnp.sqrt(spread[:, None] + 1e-05)
    return (normed * norm_gain[None] + norm_bias[None]).astype(jnp.bfloat16)


def solution(mesh):
    in_specs = (
        P("seq", "tp"),
        P(None, "tp"),
        P(None, "tp"),
        P(None, "tp"),
        P(None, "tp"),
        P("tp", None),
        P("tp", None),
        P("tp", None),
        P("tp"),
        P("tp"),
    )
    out_specs = P("seq", "tp")
    return jax.shard_map(shards, mesh=mesh, in_specs=in_specs, out_specs=out_specs, check_vma=False)
```

profile of v0, /device:TPU:0, one launch (start us, length us, event | category | flops | bytes accessed | tf_op | source)
XLA Modules:
  0.0 256.7 jit_solution(2363888968351827985)
XLA Ops:
  6.5 0.7 all-gather.2.cloned.1.call-update
  7.3 0.0 reduce-scatter.2.cloned.1.call-start
  7.4 0.6 fusion.10
  8.0 23.2 %fusion.3 = (bf16[1536,1024]{1,0:T(8,128)(2,1)S(1)}, bf16[1536,1024]{1,0:T(8,128)(2,1)S(1)}) fusion(f32[1024]{0:T(1024)S(1)} %multiply_exponential_fusion, f32[1536]{0:T(1024)S(1)} %subtract_convert_fusion), kind=kLoop, calls=%fused_computation.8 | loop fusion | flops 4718592 | bytes 6301696 | tf_op jit(solution)/shard_map/convert.1
  31.2 4.8 %fusion.11 = bf16[1536,512]{0,1:T(8,128)(2,1)} fusion(bf16[2048,512]{1,0:T(8,128)(2,1)S(1)} %copy-done.7, bf16[1536,1024]{1,0:T(8,128)(2,1)S(1)} %get-tuple-element.6, bf16[1536,1024]{1,0:T(8,128)(2,1)S(1)} %get-tuple-element.5), kind=kOutput, calls=%fused_computation.17 | convolution fusion | flops 3234594816 | bytes 9961472 | tf_op jit(solution)/shard_map/dot_general | solution.py:51
  36.1 21.3 %all-gather.2.cloned.1.call-done = bf16[512,2048]{1,0:T(8,128)(2,1)} async-done(((bf16[512,512]{1,0:T(8,128)(2,1)}), bf16[512,2048]{1,0:T(8,128)(2,1)}) %all-gather.2.cloned.1.call-update) | async-done | bytes 2097168 | tf_op jit(solution)/shard_map/all_gather | solution.py:39
  57.3 3.6 %convolution_convert_fusion.1 = bf16[512,512]{1,0:T(8,128)(2,1)S(1)} fusion(bf16[512,2048]{1,0:T(8,128)(2,1)} %all-gather.2.cloned.1.call-done, bf16[2048,512]{1,0:T(8,128)(2,1)} %param.12), kind=kOutput, calls=%fused_computation.23 | convolution fusion | flops 1074003968 | bytes 4718592 | tf_op jit(solution)/shard_map/dot_general | solution.py:41
  61.0 4.3 %collective-permute-start.2 = (bf16[512,512]{1,0:T(8,128)(2,1)S(1)}, bf16[512,512]{1,0:T(8,128)(2,1)}, u32[]{:S(2)}, u32[]{:S(2)}) collective-permute-start(bf16[512,512]{1,0:T(8,128)(2,1)S(1)} %convolution_convert_fusion.1), channel_id=1, source_target_pairs={{0,8},{4,12},{8,16},{12,20},{16,24},{20,28},{1,9},{5,13},{9,17},{1... | collective-permute-start | bytes 1572872 | tf_op jit(solution)/shard_map/ppermute | solution.py:10
  65.3 2.1 collective-permute-start.3
  67.4 2.0 convolution_convert_fusion.3
  69.4 3.3 %collective-permute-start = (bf16[512,512]{1,0:T(8,128)(2,1)}, bf16[512,512]{1,0:T(8,128)(2,1)}, u32[]{:S(2)}, u32[]{:S(2)}) collective-permute-start(bf16[512,512]{1,0:T(8,128)(2,1)} %convolution_convert_fusion.3), channel_id=1, source_target_pairs={{0,8},{4,12},{8,16},{12,20},{16,24},{20,28},{1,9},{5,13},{9,17},{1... | collective-permute-start | bytes 1572872 | tf_op jit(solution)/shard_map/ppermute | solution.py:10
  72.8 4.0 %collective-permute-start.1 = (bf16[512,512]{1,0:T(8,128)(2,1)}, bf16[512,512]{1,0:T(8,128)(2,1)}, u32[]{:S(2)}, u32[]{:S(2)}) collective-permute-start(bf16[512,512]{1,0:T(8,128)(2,1)} %convolution_convert_fusion.3), channel_id=1, source_target_pairs={{0,4},{4,8},{8,12},{12,16},{16,20},{20,24},{24,28},{1,5},{5,9},{9,... | collective-permute-start | bytes 1572872 | tf_op jit(solution)/shard_map/ppermute | solution.py:10
  76.8 2.1 convolution_convert_fusion.2
  78.9 2.2 copy.16
  81.1 8.1 %fusion.19 = f32[4,512,1536]{2,1,0:T(8,128)} fusion(bf16[1536,4,128]{0,2,1:T(8,128)(2,1)} %bitcast.35, f32[512,4,128]{2,0,1:T(8,128)} %copy.16, f32[4,128]{1,0:T(4,128)S(1)} %copy-done.3), kind=kOutput, calls=%fused_computation.34 | convolution fusion | flops 805830656 | bytes 15206400 | tf_op jit(solution)/shard_map/ihd,ehd->hie/dot_general | solution.py:61
  89.2 10.7 %pad.4 = f32[4,512,1537]{2,1,0:T(8,128)} pad(f32[4,512,1536]{2,1,0:T(8,128)} %fusion.19, f32[]{:T(128)} %constant.13.clone.1), padding=0_0x0_0x0_1 | pad | bytes 25174020 | tf_op jit(solution)/shard_map/jit(_pad)/pad | solution.py:23
  99.9 20.2 %reshape.101 = f32[3147776]{0:T(1024)} reshape(f32[4,512,1537]{2,1,0:T(8,128)} %pad.4) | data formatting | bytes 25182208
  120.1 15.0 %reshape.96 = f32[4,786944]{1,0:T(4,128)} reshape(f32[3147776]{0:T(1024)} %reshape.101) | data formatting | bytes 25182208 | tf_op jit(solution)/shard_map/reshape | solution.py:24
  135.1 9.7 %slice.4 = f32[4,786432]{1,0:T(4,128)S(1)} slice(f32[4,786944]{1,0:T(4,128)} %reshape.96), slice={[0:4], [511:786943]} | slice | bytes 25165824 | tf_op jit(solution)/shard_map/slice | solution.py:25
  144.8 11.5 %fusion.2 = f32[4,512,1536]{2,1,0:T(8,128)} fusion(f32[1,4,512,1536]{3,1,2,0:T(4,128)S(1)} %bitcast.34, pred[512,1536]{1,0:T(8,128)(4,1)S(1)} %fusion.10, f32[512,4,128]{2,0,1:T(8,128)S(1)} %copy-done.1, f32[4,128]{1,0:T(4,128)S(1)} %copy-done.4, bf16[512,512]{1,0:T(8,128)(2,1)S(1)} %convolution_convert_fusion.1, ...), kind=kOutput, calls=%fused_computation.3 | convolution fusion | flops 819986432 | bytes 28575744 | tf_op jit(solution)/shard_map/ihd,jhd->hij/dot_general | solution.py:60
  156.3 10.4 %fusion.24 = f32[4,512]{1,0:T(4,128)S(1)} fusion(f32[4,512,1536]{2,1,0:T(8,128)} %fusion.2), kind=kOutput, calls=%fused_computation.45 | output fusion | flops 6292991 | bytes 12591104 | tf_op jit(solution)/shard_map/sub | solution.py:68
  166.8 2.6 %pad_maximum_fusion = bf16[1536,512]{1,0:T(8,128)(2,1)} fusion(bf16[512,512]{1,0:T(8,128)(2,1)} %convolution_convert_fusion.3, bf16[512,512]{1,0:T(8,128)(2,1)} %collective-permute-done.1, bf16[512,512]{1,0:T(8,128)(2,1)} %collective-permute-done), kind=kLoop, calls=%fused_computation.21 | loop fusion | flops 4718592 | bytes 3145728 | tf_op jit(solution)/shard_map/concatenate | solution.py:50
  169.4 2.6 %copy.22 = bf16[1536,512]{0,1:T(8,128)(2,1)} copy(bf16[1536,512]{1,0:T(8,128)(2,1)} %pad_maximum_fusion) | data formatting | bytes 3145728 | tf_op jit(solution)/shard_map/reshape | solution.py:56
  172.0 10.9 %fusion.16 = bf16[4,128,512]{2,1,0:T(8,128)(2,1)S(1)} fusion(bf16[1536,4,128]{0,2,1:T(8,128)(2,1)} %bitcast.36, f32[4,512]{1,0:T(4,128)S(1)} %fusion.24, f32[4,512,1536]{2,1,0:T(8,128)} %fusion.2), kind=kOutput, calls=%fused_computation.26 | convolution fusion | flops 815009280 | bytes 14688256 | tf_op jit(solution)/shard_map/hij,jhd->ihd/dot_general | solution.py:69
  182.9 2.6 %convolution_convert_fusion = bf16[512,2048]{1,0:T(8,128)(2,1)} fusion(bf16[512,512]{0,1:T(8,128)(2,1)S(1)} %bitcast.38, bf16[512,2048]{1,0:T(8,128)(2,1)S(1)} %copy-done), kind=kOutput, calls=%fused_computation.18 | convolution fusion | flops 1074790400 | bytes 4718592 | tf_op jit(solution)/shard_map/dot_general | solution.py:71
  185.6 0.0 reduce-scatter.2.cloned.1.call-update
  185.6 40.8 %reduce-scatter.2.cloned.1.call-done = bf16[512,512]{1,0:T(8,128)(2,1)} async-done(((bf16[512,2048]{1,0:T(8,128)(2,1)}), bf16[512,512]{1,0:T(8,128)(2,1)}) %reduce-scatter.2.cloned.1.call-update) | async-done | bytes 524304 | tf_op jit(solution)/shard_map/reduce_scatter | solution.py:72
  226.4 1.3 fusion.18
  227.6 10.2 %psum.14 = f32[512]{0:T(512)S(1)} all-reduce(f32[512]{0:T(512)S(1)} %fusion.18), channel_id=1, replica_groups=mesh['seq'=8,'tp'=4] {'tp'}, use_global_device_ids=true, to_apply=%region_4.5 | all-reduce | flops 512 | bytes 4096 | tf_op jit(solution)/shard_map/psum | solution.py:76
  237.8 1.3 multiply_reduce_fusion
  239.1 8.6 %psum.15 = f32[512]{0:T(512)S(1)} all-reduce(f32[512]{0:T(512)S(1)} %multiply_reduce_fusion), channel_id=1, replica_groups=mesh['seq'=8,'tp'=4] {'tp'}, use_global_device_ids=true, to_apply=%region_6.7 | all-reduce | flops 512 | bytes 4096 | tf_op jit(solution)/shard_map/psum | solution.py:79
  247.7 2.1 add_convert_fusion
  (33 shorter events, 0.1 us)
Async XLA Ops:
  6.5 176.4 %copy-start = (bf16[512,2048]{1,0:T(8,128)(2,1)S(1)}, bf16[512,2048]{1,0:T(8,128)(2,1)}, u32[]{:S(2)}) copy-start(bf16[512,2048]{1,0:T(8,128)(2,1)} %param.15) | copy-start | bytes 6291460
  6.5 50.8 %all-gather.2.cloned.1.call-start = ((), (), s32[]{:S(2)}) async-start(), calls=%async_computation.1 | async-start | bytes 2621440 | tf_op jit(solution)/shard_map/all_gather | solution.py:39
  7.3 219.1 %reduce-scatter.2.cloned.1.call-start = ((), (), s32[]{:S(2)}) async-start(), calls=%async_computation.2 | async-start | bytes 2621440 | tf_op jit(solution)/shard_map/reduce_scatter | solution.py:72
  7.9 23.3 %copy-start.7 = (bf16[2048,512]{1,0:T(8,128)(2,1)S(1)}, bf16[2048,512]{1,0:T(8,128)(2,1)}, u32[]{:S(2)}) copy-start(bf16[2048,512]{1,0:T(8,128)(2,1)} %param.14) | copy-start | bytes 6291460
  57.3 10.1 %copy-start.8 = (bf16[2048,512]{1,0:T(8,128)(2,1)S(1)}, bf16[2048,512]{1,0:T(8,128)(2,1)}, u32[]{:S(2)}) copy-start(bf16[2048,512]{1,0:T(8,128)(2,1)} %param.13) | copy-start | bytes 6291460
  57.3 10.1 %copy-start.10 = (bf16[512,2048]{1,0:T(8,128)(2,1)S(1)}, bf16[512,2048]{1,0:T(8,128)(2,1)}, u32[]{:S(2)}) copy-start(bf16[512,2048]{1,0:T(8,128)(2,1)} %all-gather.2.cloned.1.call-done) | copy-start | bytes 6291460
  61.0 15.8 %copy-start.9 = (bf16[2048,512]{1,0:T(8,128)(2,1)S(1)}, bf16[2048,512]{1,0:T(8,128)(2,1)}, u32[]{:S(2)}) copy-start(bf16[2048,512]{1,0:T(8,128)(2,1)} %param.11) | copy-start | bytes 6291460
  61.0 83.8 %collective-permute-start.2 = (bf16[512,512]{1,0:T(8,128)(2,1)S(1)}, bf16[512,512]{1,0:T(8,128)(2,1)}, u32[]{:S(2)}, u32[]{:S(2)}) collective-permute-start(bf16[512,512]{1,0:T(8,128)(2,1)S(1)} %convolution_convert_fusion.1), channel_id=1, source_target_pairs={{0,8},{4,12},{8,16},{12,20},{16,24},{20,28},{1,9},{5,13},{9,17},{1... | collective-permute-start | bytes 1572872 | tf_op jit(solution)/shard_map/ppermute | solution.py:10
  65.3 79.5 %collective-permute-start.3 = (bf16[512,512]{1,0:T(8,128)(2,1)S(1)}, bf16[512,512]{1,0:T(8,128)(2,1)}, u32[]{:S(2)}, u32[]{:S(2)}) collective-permute-start(bf16[512,512]{1,0:T(8,128)(2,1)S(1)} %convolution_convert_fusion.1), channel_id=1, source_target_pairs={{0,4},{4,8},{8,12},{12,16},{16,20},{20,24},{24,28},{1,5},{5,9},{9,... | collective-permute-start | bytes 1572872 | tf_op jit(solution)/shard_map/ppermute | solution.py:10
  69.4 11.7 %copy-start.3 = (f32[4,128]{1,0:T(4,128)S(1)}, f32[4,128]{1,0:T(4,128)}, u32[]{:S(2)}) copy-start(f32[4,128]{1,0:T(4,128)} %param.17) | copy-start | bytes 6148
  69.4 97.3 %collective-permute-start = (bf16[512,512]{1,0:T(8,128)(2,1)}, bf16[512,512]{1,0:T(8,128)(2,1)}, u32[]{:S(2)}, u32[]{:S(2)}) collective-permute-start(bf16[512,512]{1,0:T(8,128)(2,1)} %convolution_convert_fusion.3), channel_id=1, source_target_pairs={{0,8},{4,12},{8,16},{12,20},{16,24},{20,28},{1,9},{5,13},{9,17},{1... | collective-permute-start | bytes 1572872 | tf_op jit(solution)/shard_map/ppermute | solution.py:10
  72.8 94.0 %collective-permute-start.1 = (bf16[512,512]{1,0:T(8,128)(2,1)}, bf16[512,512]{1,0:T(8,128)(2,1)}, u32[]{:S(2)}, u32[]{:S(2)}) collective-permute-start(bf16[512,512]{1,0:T(8,128)(2,1)} %convolution_convert_fusion.3), channel_id=1, source_target_pairs={{0,4},{4,8},{8,12},{12,16},{16,20},{20,24},{24,28},{1,5},{5,9},{9,... | collective-permute-start | bytes 1572872 | tf_op jit(solution)/shard_map/ppermute | solution.py:10
  135.1 9.7 %copy-start.1 = (f32[512,4,128]{2,0,1:T(8,128)S(1)}, f32[512,4,128]{2,0,1:T(8,128)}, u32[]{:S(2)}) copy-start(f32[512,4,128]{2,0,1:T(8,128)} %copy.16) | copy-start | bytes 3145732
  135.1 9.7 %copy-start.4 = (f32[4,128]{1,0:T(4,128)S(1)}, f32[4,128]{1,0:T(4,128)}, u32[]{:S(2)}) copy-start(f32[4,128]{1,0:T(4,128)} %param.16) | copy-start | bytes 6148
  182.9 43.4 %copy-start.2 = (bf16[512,512]{1,0:T(8,128)(2,1)S(1)}, bf16[512,512]{1,0:T(8,128)(2,1)}, u32[]{:S(2)}) copy-start(bf16[512,512]{1,0:T(8,128)(2,1)} %param.10) | copy-start | bytes 1572868
  185.6 62.1 %copy-start.5 = (f32[512]{0:T(512)S(1)}, f32[512]{0:T(512)}, u32[]{:S(2)}) copy-start(f32[512]{0:T(512)} %param.19) | copy-start | bytes 6148
  185.6 62.1 %copy-start.6 = (f32[512]{0:T(512)S(1)}, f32[512]{0:T(512)}, u32[]{:S(2)}) copy-start(f32[512]{0:T(512)} %param.18) | copy-start | bytes 6148
Sparse Core Ops, SparseCore 0:
  8.9 48.3 all-gather.1
  185.7 40.5 reduce-scatter.1
where the time goes:
time: 257 us
  waiting for transfers between devices  62.8 us (24%)
  local copies, waits for them, and re-layouts  60.4 us (24%)
  matrix products  45.7 us (18%)
  other arithmetic  41.6 us (16%)
  blocking collectives  18.7 us (7%)
  starting transfers between devices  13.8 us (5%)
  between operations  13.6 us (5%)
    reduce_scatter x1, waiting for transfers between devices, shards(): lax.psum_scatter(partial_out.astype(jnp.bfloat16), 'tp', scatter_dimensio...  40.8 us
    another operation x1, other arithmetic  23.2 us
    all_gather x1, waiting for transfers between devices, shards(): own = lax.all_gather(hidden_in, 'tp', axis=1, tiled=True)  21.3 us
    unnamed x23, local copies, waits for them, and re-layouts  20.3 us
    reshape x1, local copies, waits for them, and re-layouts, shift_rows(): flat = padded.reshape(heads, seg * (span + 1))  15 us
    ppermute x4, starting transfers between devices, shifted(): return lax.ppermute(block, axis, route)  13.8 us
    dot_general x1, matrix products, shards(): jnp.einsum('ihd,jhd->hij', content_q, keys, preferred_element_type=jnp.fl...  11.5 us
    dot_general x1, matrix products, shards(): jnp.einsum('hij,jhd->ihd', probs, values, preferred_element_type=jnp.floa...  10.9 us
  transfers between devices with their start and end apart: 6, of which 2 were waited for; matrix products, arithmetic and copies ran while one was open for 47% of the time, Pallas kernels for 0%

commit v1 on v0

--- a/solution.py
+++ b/solution.py
@@ -36,7 +36,12 @@
     span = 3 * seg
     memory = 2 * seg
     place = lax.axis_index("seq")
-    own = lax.all_gather(hidden_in, "tp", axis=1, tiled=True)
+    ring = [hidden_in]
+    for hop in range(3):
+        ring.append(lax.ppermute(ring[-1], "tp", [(dev, (dev + 1) % 4) for dev in range(4)]))
+    own = jnp.roll(
+        jnp.concatenate(ring[::-1], axis=1), (lax.axis_index("tp") + 1) * ring[0].shape[1], axis=1
+    )
     query = jnp.dot(own, w_query, preferred_element_type=jnp.float32).astype(jnp.bfloat16)
     own_keys = jnp.dot(own, w_key, preferred_element_type=jnp.float32).astype(jnp.bfloat16)
     own_values = jnp.dot(own, w_value, preferred_element_type=jnp.float32).astype(jnp.bfloat16)

time: 257 us -> 274 us (1.066)
  local copies, waits for them, and re-layouts: 60.4 us -> 69.8 us
  starting transfers between devices: 13.8 us -> 17.7 us
  matrix products: 45.7 us -> 48.8 us
    ppermute x0 -> x3, waiting for transfers between devices: none -> 22.8 us  [shards(): lax.ppermute(ring[-1], 'tp', [(dev, (dev + 1) % 4) for dev in range(4)])]
    all_gather x1 -> x0, waiting for transfers between devices: 21.3 us -> none  [shards(): own = lax.all_gather(hidden_in, 'tp', axis=1, tiled=True)]
    unnamed x23 -> x32, local copies, waits for them, and re-layouts: 20.3 us -> 25.8 us
    ppermute x0 -> x3, starting transfers between devices: none -> 4.68 us  [shards(): lax.ppermute(ring[-1], 'tp', [(dev, (dev + 1) % 4) for dev in range(4)])]
    dot_general x1, matrix products: 11.5 us -> 16 us  [shards(): jnp.einsum('ihd,jhd->hij', content_q, keys, preferred_element_type=jnp.fl...]
    slice x1, local copies, waits for them, and re-layouts: 9.66 us -> 13.3 us  [shift_rows(): return flat[:, seg - 1:seg - 1 + seg * span].reshape(heads, seg, span)]
  transfers between devices with their start and end apart: 6 -> 8, of which waited for: 2 -> 3; matrix products, arithmetic and copies ran while one was open for 47% -> 39% of each run, Pallas kernels for 0% -> 0%
where the time goes in v1:
time: 274 us; the launch traced here: 273 us
  local copies, waits for them, and re-layouts  69.8 us (25%)
  waiting for transfers between devices  62.5 us (23%)
  matrix products  48.8 us (18%)
  other arithmetic  41.6 us (15%)
  blocking collectives  18.7 us (7%)
  starting transfers between devices  17.7 us (6%)
  between operations  13.6 us (5%)
    reduce_scatter x1, waiting for transfers between devices, shards(): lax.psum_scatter(partial_out.astype(jnp.bfloat16), 'tp', scatter_dimensio...  39.6 us
    unnamed x32, local copies, waits for them, and re-layouts  25.8 us
    another operation x1, other arithmetic  23.2 us
    ppermute x3, waiting for transfers between devices, shards(): lax.ppermute(ring[-1], 'tp', [(dev, (dev + 1) % 4) for dev in range(4)])  22.8 us
    dot_general x1, matrix products, shards(): jnp.einsum('ihd,jhd->hij', content_q, keys, preferred_element_type=jnp.fl...  16 us
    reshape x1, local copies, waits for them, and re-layouts, shift_rows(): flat = padded.reshape(heads, seg * (span + 1))  15 us
    slice x1, local copies, waits for them, and re-layouts, shift_rows(): return flat[:, seg - 1:seg - 1 + seg * span].reshape(heads, seg, span)  13.3 us
    ppermute x4, starting transfers between devices, shifted(): return lax.ppermute(block, axis, route)  13 us
  transfers between devices with their start and end apart: 8, of which 3 were waited for; matrix products, arithmetic and copies ran while one was open for 39% of the time, Pallas kernels for 0%

profile of v1, /device:TPU:0, one launch (start us, length us, event | category | flops | bytes accessed | tf_op | source)
XLA Modules:
  0.0 272.9 jit_solution(7249034505649833546)
XLA Ops:
  6.5 3.1 %collective-permute-start = (bf16[512,512]{1,0:T(8,128)(2,1)}, bf16[512,512]{1,0:T(8,128)(2,1)S(1)}, u32[]{:S(2)}, u32[]{:S(2)}) collective-permute-start(bf16[512,512]{1,0:T(8,128)(2,1)} %param.10), channel_id=1, source_target_pairs={{0,1},{1,2},{2,3},{3,0},{4,5},{5,6},{6,7},{7,4},{8,9},{9,10},{10,1... | collective-permute-start | bytes 1572872 | tf_op jit(solution)/shard_map/ppermute | solution.py:41
  9.6 23.2 %fusion.3 = (bf16[1536,1024]{1,0:T(8,128)(2,1)S(1)}, bf16[1536,1024]{1,0:T(8,128)(2,1)S(1)}) fusion(f32[1024]{0:T(1024)S(1)} %multiply_exponential_fusion, f32[1536]{0:T(1024)S(1)} %subtract_convert_fusion), kind=kLoop, calls=%fused_computation.8 | loop fusion | flops 4718592 | bytes 6301696 | tf_op jit(solution)/shard_map/convert.1
  32.9 1.6 collective-permute-start.1
  34.5 4.9 %fusion.11 = bf16[1536,512]{0,1:T(8,128)(2,1)} fusion(bf16[2048,512]{1,0:T(8,128)(2,1)S(1)} %copy-done.8, bf16[1536,1024]{1,0:T(8,128)(2,1)S(1)} %get-tuple-element.6, bf16[1536,1024]{1,0:T(8,128)(2,1)S(1)} %get-tuple-element.5), kind=kOutput, calls=%fused_computation.17 | convolution fusion | flops 3234594816 | bytes 9961472 | tf_op jit(solution)/shard_map/dot_general | solution.py:56
  39.4 8.8 %collective-permute-done.1 = bf16[512,512]{1,0:T(8,128)(2,1)} collective-permute-done((bf16[512,512]{1,0:T(8,128)(2,1)S(1)}, bf16[512,512]{1,0:T(8,128)(2,1)}, u32[]{:S(2)}, u32[]{:S(2)}) %collective-permute-start.1) | collective-permute-done | bytes 524320 | tf_op jit(solution)/shard_map/ppermute | solution.py:41
  48.9 14.0 %collective-permute-done.2 = bf16[512,512]{1,0:T(8,128)(2,1)} collective-permute-done((bf16[512,512]{1,0:T(8,128)(2,1)}, bf16[512,512]{1,0:T(8,128)(2,1)}, u32[]{:S(2)}, u32[]{:S(2)}) %collective-permute-start.2) | collective-permute-done | bytes 524320 | tf_op jit(solution)/shard_map/ppermute | solution.py:41
  65.1 1.1 constant_dynamic-update-slice_fusion.5
  68.6 2.0 fusion.22
  70.7 2.2 collective-permute-start.4
  72.9 4.1 %collective-permute-start.3 = (bf16[512,512]{1,0:T(8,128)(2,1)}, bf16[512,512]{1,0:T(8,128)(2,1)}, u32[]{:S(2)}, u32[]{:S(2)}) collective-permute-start(bf16[512,512]{1,0:T(8,128)(2,1)} %fusion.22), channel_id=1, source_target_pairs={{0,8},{4,12},{8,16},{12,20},{16,24},{20,28},{1,9},{5,13},{9,17},{1... | collective-permute-start | bytes 1572872 | tf_op jit(solution)/shard_map/ppermute | solution.py:10
  77.0 2.1 fusion.28
  79.0 4.1 %collective-permute-start.6 = (bf16[512,512]{1,0:T(8,128)(2,1)}, bf16[512,512]{1,0:T(8,128)(2,1)}, u32[]{:S(2)}, u32[]{:S(2)}) collective-permute-start(bf16[512,512]{1,0:T(8,128)(2,1)} %fusion.28), channel_id=1, source_target_pairs={{0,4},{4,8},{8,12},{12,16},{16,20},{20,24},{24,28},{1,5},{5,9},{9,... | collective-permute-start | bytes 1572872 | tf_op jit(solution)/shard_map/ppermute | solution.py:10
  83.2 2.6 collective-permute-start.5
  85.8 2.1 fusion.25
  87.9 2.2 copy.16
  90.1 8.1 %fusion.34 = f32[4,512,1536]{2,1,0:T(8,128)} fusion(bf16[1536,4,128]{0,2,1:T(8,128)(2,1)} %bitcast.32, f32[512,4,128]{2,0,1:T(8,128)} %copy.16, f32[4,128]{1,0:T(4,128)S(1)} %copy-done.4), kind=kOutput, calls=%fused_computation.40 | convolution fusion | flops 805830656 | bytes 15206400 | tf_op jit(solution)/shard_map/ihd,ehd->hie/dot_general | solution.py:66
  98.2 10.8 %pad.4 = f32[4,512,1537]{2,1,0:T(8,128)} pad(f32[4,512,1536]{2,1,0:T(8,128)} %fusion.34, f32[]{:T(128)} %constant.59.clone.1), padding=0_0x0_0x0_1 | pad | bytes 25174020 | tf_op jit(solution)/shard_map/jit(_pad)/pad | solution.py:23
  109.0 20.2 %reshape.101 = f32[3147776]{0:T(1024)} reshape(f32[4,512,1537]{2,1,0:T(8,128)} %pad.4) | data formatting | bytes 25182208
  129.1 15.0 %reshape.96 = f32[4,786944]{1,0:T(4,128)} reshape(f32[3147776]{0:T(1024)} %reshape.101) | data formatting | bytes 25182208 | tf_op jit(solution)/shard_map/reshape | solution.py:24
  144.2 13.3 %slice.4 = f32[4,786432]{1,0:T(4,128)} slice(f32[4,786944]{1,0:T(4,128)} %reshape.96), slice={[0:4], [511:786943]} | slice | bytes 25165824 | tf_op jit(solution)/shard_map/slice | solution.py:25
  157.5 2.6 pad_maximum_fusion
  160.1 2.6 copy.22
  162.8 16.0 %fusion.2 = f32[4,512,1536]{2,1,0:T(8,128)} fusion(f32[1,4,512,1536]{3,1,2,0:T(4,128)} %bitcast.31, pred[512,1536]{1,0:T(8,128)(4,1)S(1)} %fusion.10, f32[512,4,128]{2,0,1:T(8,128)} %copy.16, f32[4,128]{1,0:T(4,128)S(1)} %copy-done.5, bf16[512,512]{1,0:T(8,128)(2,1)} %fusion.28, bf16[512,512]{1,0:T(8,128)(2,1)} %collective-permute-done.6, ...), kind=kOutput, calls=%fused_computation.3 | convolution fusion | flops 819986432 | bytes 28575744 | tf_op jit(solution)/shard_map/ihd,jhd->hij/dot_general | solution.py:65
  178.8 10.5 %fusion.42 = f32[4,512]{1,0:T(4,128)S(1)} fusion(f32[4,512,1536]{2,1,0:T(8,128)} %fusion.2), kind=kOutput, calls=%fused_computation.62 | output fusion | flops 6292991 | bytes 12591104 | tf_op jit(solution)/shard_map/sub | solution.py:73
  189.2 11.0 %fusion.31 = bf16[4,128,512]{2,1,0:T(8,128)(2,1)S(1)} fusion(bf16[1536,4,128]{0,2,1:T(8,128)(2,1)} %bitcast.33, f32[4,512]{1,0:T(4,128)S(1)} %fusion.42, f32[4,512,1536]{2,1,0:T(8,128)} %fusion.2), kind=kOutput, calls=%fused_computation.32 | convolution fusion | flops 815009280 | bytes 14688256 | tf_op jit(solution)/shard_map/hij,jhd->ihd/dot_general | solution.py:74
  200.3 2.6 convolution_convert_fusion
  203.0 39.6 %reduce-scatter.2.cloned.1.call-done = bf16[512,512]{1,0:T(8,128)(2,1)} async-done(((bf16[512,2048]{1,0:T(8,128)(2,1)}), bf16[512,512]{1,0:T(8,128)(2,1)}) %reduce-scatter.2.cloned.1.call-update) | async-done | bytes 524304 | tf_op jit(solution)/shard_map/reduce_scatter | solution.py:77
  242.6 1.2 fusion.33
  243.9 10.2 %psum.14 = f32[512]{0:T(512)S(1)} all-reduce(f32[512]{0:T(512)S(1)} %fusion.33), channel_id=1, replica_groups=mesh['seq'=8,'tp'=4] {'tp'}, use_global_device_ids=true, to_apply=%region_4.5 | all-reduce | flops 512 | bytes 4096 | tf_op jit(solution)/shard_map/psum | solution.py:81
  254.0 1.3 multiply_reduce_fusion
  255.4 8.6 %psum.15 = f32[512]{0:T(512)S(1)} all-reduce(f32[512]{0:T(512)S(1)} %multiply_reduce_fusion), channel_id=1, replica_groups=mesh['seq'=8,'tp'=4] {'tp'}, use_global_device_ids=true, to_apply=%region_6.7 | all-reduce | flops 512 | bytes 4096 | tf_op jit(solution)/shard_map/psum | solution.py:84
  264.0 2.1 add_convert_fusion
  (46 shorter events, 5.3 us)
Async XLA Ops:
  6.5 193.7 %copy-start = (bf16[512,2048]{1,0:T(8,128)(2,1)S(1)}, bf16[512,2048]{1,0:T(8,128)(2,1)}, u32[]{:S(2)}) copy-start(bf16[512,2048]{1,0:T(8,128)(2,1)} %param.15) | copy-start | bytes 6291460
  6.5 236.1 %reduce-scatter.2.cloned.1.call-start = ((), (), s32[]{:S(2)}) async-start(), calls=%async_computation.1 | async-start | bytes 2621440 | tf_op jit(solution)/shard_map/reduce_scatter | solution.py:77
  6.5 26.3 %collective-permute-start = (bf16[512,512]{1,0:T(8,128)(2,1)}, bf16[512,512]{1,0:T(8,128)(2,1)S(1)}, u32[]{:S(2)}, u32[]{:S(2)}) collective-permute-start(bf16[512,512]{1,0:T(8,128)(2,1)} %param.10), channel_id=1, source_target_pairs={{0,1},{1,2},{2,3},{3,0},{4,5},{5,6},{6,7},{7,4},{8,9},{9,10},{10,1... | collective-permute-start | bytes 1572872 | tf_op jit(solution)/shard_map/ppermute | solution.py:41
  9.6 24.9 %copy-start.8 = (bf16[2048,512]{1,0:T(8,128)(2,1)S(1)}, bf16[2048,512]{1,0:T(8,128)(2,1)}, u32[]{:S(2)}) copy-start(bf16[2048,512]{1,0:T(8,128)(2,1)} %param.14) | copy-start | bytes 6291460
  32.9 6.5 %copy-start.2 = (bf16[512,512]{1,0:T(8,128)(2,1)}, bf16[512,512]{1,0:T(8,128)(2,1)S(1)}, u32[]{:S(2)}) copy-start(bf16[512,512]{1,0:T(8,128)(2,1)S(1)} %collective-permute-done) | copy-start | bytes 1572868
  32.9 15.3 %collective-permute-start.1 = (bf16[512,512]{1,0:T(8,128)(2,1)S(1)}, bf16[512,512]{1,0:T(8,128)(2,1)}, u32[]{:S(2)}, u32[]{:S(2)}) collective-permute-start(bf16[512,512]{1,0:T(8,128)(2,1)S(1)} %collective-permute-done), channel_id=1, source_target_pairs={{0,1},{1,2},{2,3},{3,0},{4,5},{5,6},{6,7},{7,4},{8,9},{9,10},{10,1... | collective-permute-start | bytes 1572872 | tf_op jit(solution)/shard_map/ppermute | solution.py:41
  39.4 26.8 %copy-start.1 = (bf16[512,512]{1,0:T(8,128)(2,1)S(1)}, bf16[512,512]{1,0:T(8,128)(2,1)}, u32[]{:S(2)}) copy-start(bf16[512,512]{1,0:T(8,128)(2,1)} %param.10) | copy-start | bytes 1572868
  48.2 14.6 %collective-permute-start.2 = (bf16[512,512]{1,0:T(8,128)(2,1)}, bf16[512,512]{1,0:T(8,128)(2,1)}, u32[]{:S(2)}, u32[]{:S(2)}) collective-permute-start(bf16[512,512]{1,0:T(8,128)(2,1)} %collective-permute-done.1), channel_id=1, source_target_pairs={{0,1},{1,2},{2,3},{3,0},{4,5},{5,6},{6,7},{7,4},{8,9},{9,10},{10,1... | collective-permute-start | bytes 1572872 | tf_op jit(solution)/shard_map/ppermute | solution.py:41
  48.3 20.2 %copy-start.3 = (bf16[512,512]{1,0:T(8,128)(2,1)S(1)}, bf16[512,512]{1,0:T(8,128)(2,1)}, u32[]{:S(2)}) copy-start(bf16[512,512]{1,0:T(8,128)(2,1)} %copy-done.2) | copy-start | bytes 1572868
  48.8 19.8 %copy-start.9 = (bf16[2048,512]{1,0:T(8,128)(2,1)S(1)}, bf16[2048,512]{1,0:T(8,128)(2,1)}, u32[]{:S(2)}) copy-start(bf16[2048,512]{1,0:T(8,128)(2,1)} %param.13) | copy-start | bytes 6291460
  68.5 8.4 %copy-start.10 = (bf16[2048,512]{1,0:T(8,128)(2,1)S(1)}, bf16[2048,512]{1,0:T(8,128)(2,1)}, u32[]{:S(2)}) copy-start(bf16[2048,512]{1,0:T(8,128)(2,1)} %param.12) | copy-start | bytes 6291460
  70.7 15.1 %copy-start.11 = (bf16[2048,512]{1,0:T(8,128)(2,1)S(1)}, bf16[2048,512]{1,0:T(8,128)(2,1)}, u32[]{:S(2)}) copy-start(bf16[2048,512]{1,0:T(8,128)(2,1)} %param.11) | copy-start | bytes 6291460
  70.7 86.8 %collective-permute-start.4 = (bf16[512,512]{1,0:T(8,128)(2,1)}, bf16[512,512]{1,0:T(8,128)(2,1)}, u32[]{:S(2)}, u32[]{:S(2)}) collective-permute-start(bf16[512,512]{1,0:T(8,128)(2,1)} %fusion.22), channel_id=1, source_target_pairs={{0,4},{4,8},{8,12},{12,16},{16,20},{20,24},{24,28},{1,5},{5,9},{9,... | collective-permute-start | bytes 1572872 | tf_op jit(solution)/shard_map/ppermute | solution.py:10
  72.9 84.6 %collective-permute-start.3 = (bf16[512,512]{1,0:T(8,128)(2,1)}, bf16[512,512]{1,0:T(8,128)(2,1)}, u32[]{:S(2)}, u32[]{:S(2)}) collective-permute-start(bf16[512,512]{1,0:T(8,128)(2,1)} %fusion.22), channel_id=1, source_target_pairs={{0,8},{4,12},{8,16},{12,20},{16,24},{20,28},{1,9},{5,13},{9,17},{1... | collective-permute-start | bytes 1572872 | tf_op jit(solution)/shard_map/ppermute | solution.py:10
  79.0 11.1 %copy-start.4 = (f32[4,128]{1,0:T(4,128)S(1)}, f32[4,128]{1,0:T(4,128)}, u32[]{:S(2)}) copy-start(f32[4,128]{1,0:T(4,128)} %param.17) | copy-start | bytes 6148
  79.0 83.7 %collective-permute-start.6 = (bf16[512,512]{1,0:T(8,128)(2,1)}, bf16[512,512]{1,0:T(8,128)(2,1)}, u32[]{:S(2)}, u32[]{:S(2)}) collective-permute-start(bf16[512,512]{1,0:T(8,128)(2,1)} %fusion.28), channel_id=1, source_target_pairs={{0,4},{4,8},{8,12},{12,16},{16,20},{20,24},{24,28},{1,5},{5,9},{9,... | collective-permute-start | bytes 1572872 | tf_op jit(solution)/shard_map/ppermute | solution.py:10
  83.2 79.6 %collective-permute-start.5 = (bf16[512,512]{1,0:T(8,128)(2,1)}, bf16[512,512]{1,0:T(8,128)(2,1)}, u32[]{:S(2)}, u32[]{:S(2)}) collective-permute-start(bf16[512,512]{1,0:T(8,128)(2,1)} %fusion.28), channel_id=1, source_target_pairs={{0,8},{4,12},{8,16},{12,20},{16,24},{20,28},{1,9},{5,13},{9,17},{1... | collective-permute-start | bytes 1572872 | tf_op jit(solution)/shard_map/ppermute | solution.py:10
  157.5 5.3 %copy-start.5 = (f32[4,128]{1,0:T(4,128)S(1)}, f32[4,128]{1,0:T(4,128)}, u32[]{:S(2)}) copy-start(f32[4,128]{1,0:T(4,128)} %param.16) | copy-start | bytes 6148
  200.3 63.7 %copy-start.6 = (f32[512]{0:T(512)S(1)}, f32[512]{0:T(512)}, u32[]{:S(2)}) copy-start(f32[512]{0:T(512)} %param.19) | copy-start | bytes 6148
  200.3 63.7 %copy-start.7 = (f32[512]{0:T(512)S(1)}, f32[512]{0:T(512)}, u32[]{:S(2)}) copy-start(f32[512]{0:T(512)} %param.18) | copy-start | bytes 6148
Sparse Core Ops, SparseCore 0:
  203.1 39.4 reduce-scatter.1
